TPU v7x, 32 devices: a whole 2x2x4 slice. The times are simulated.
32 devices in a mesh: ctx: 8 (over y, x, core), head: 4 (over z).
Axes of the slice: x: 2, y: 2, z: 4, core: 2. Of those that a mesh axis runs over, the one named last changes fastest.
Arguments:
- tokens: bfloat16 [1024, 4096], P('ctx'), may hold values from -8 to 8
- w_query: bfloat16 [4096, 4096], P(None, 'head'), may hold values from -1 to 1
- w_key: bfloat16 [4096, 1024], P(None, 'head'), may hold values from -1 to 1
- w_value: bfloat16 [4096, 1024], P(None, 'head'), may hold values from -0.09375 to 0.09375
- w_out: bfloat16 [4096, 4096], P('head'), may hold values from -0.09375 to 0.09375
- doc_ids: int32 [1024], P('ctx'), may hold values from 0 to 7, never falling along the last dimension, each value on 1 to 640 neighbouring positions
Outputs:
- mixed: bfloat16 [1024, 4096], P('ctx', 'head')
Inputs may be any that keep to these rules, and one draw needn't show every extreme that they name: doc_ids never fall along the context; each document has 1 to 640 tokens and one has exactly 640.
All inputs are finite; a program needn't handle non-finite values.
Results may differ from a plain program's by a relative error of at most 0.011.
Values may be sent and summed in bfloat16 or wider, within the bound.
A program may use at most 128 MiB of HBM per device.

v0:
```python
import math

import jax
import jax.numpy as jnp
from jax import lax
from jax.sharding import PartitionSpec as P

HD = 128


def rotate(vectors, places):
    half_dim = vectors.shape[-1] // 2
    freqs = 500000.0 ** (-2.0 * jnp.arange(half_dim, dtype=jnp.float32) / vectors.shape[-1])
    angles = places.astype(jnp.float32)[:, None] * freqs[None, :]
    cosine = jnp.cos(angles)[:, None, :]
    sine = jnp.sin(angles)[:, None, :]
    first_half = vectors[..., :half_dim]
    second_half = vectors[..., half_dim:]
    return jnp.concatenate(
        [first_half * cosine - second_half * sine, second_half * cosine + first_half * sine],
        axis=-1,
    )


def shards(tokens, w_query, w_key, w_value, w_out, doc_ids):
    tok_rows = tokens.shape[0]
    my_index = lax.axis_index("ctx")
    first_row = my_index * tok_rows
    places = first_row + jnp.arange(tok_rows, dtype=jnp.int32)
    query_heads = w_query.shape[1] // HD
    kv_heads = w_key.shape[1] // HD
    group_size = query_heads // kv_heads
    queries = rotate(
        jnp.dot(tokens, w_query, preferred_element_type=jnp.float32).reshape(
            tok_rows, query_heads, HD
        ),
        places,
    ).astype(jnp.bfloat16)
    queries = queries.reshape(tok_rows, kv_heads, group_size, HD)
    keys_here = rotate(
        jnp.dot(tokens, w_key, preferred_element_type=jnp.float32).reshape(tok_rows, kv_heads, HD),
        places,
    ).astype(jnp.bfloat16)
    values_here = jnp.dot(tokens, w_value, preferred_element_type=jnp.float32).astype(jnp.bfloat16)
    kv_width = kv_heads * HD
    packed = jnp.concatenate([keys_here.reshape(tok_rows, kv_width), values_here], axis=1)
    all_docs = lax.all_gather(doc_ids, "ctx", axis=0, tiled=True)
    query_low = jnp.min(doc_ids)
    query_high = jnp.max(doc_ids)
    query_last = first_row + tok_rows - 1
    score_scale = 1.0 / math.sqrt(HD)
    initial = (
        jnp.full((kv_heads, group_size, tok_rows), -1e30, jnp.float32),
        jnp.zeros((kv_heads, group_size, tok_rows), jnp.float32),
        jnp.zeros((kv_heads, group_size, tok_rows, HD), jnp.float32),
    )
    block_kv = lax.all_gather(packed, "ctx", axis=0, tiled=True)
    key_start = jnp.int32(0)
    key_count = block_kv.shape[0]
    key_start = jnp.asarray(key_start, jnp.int32)
    key_index = jnp.arange(key_count, dtype=jnp.int32)

    def accumulate(inner):
        run_max, run_sum, run_acc = inner
        block_keys = block_kv[:, :kv_width].reshape(key_count, kv_heads, HD)
        block_values = block_kv[:, kv_width:].reshape(key_count, kv_heads, HD)
        allowed = (all_docs[None, :] == doc_ids[:, None]) & (key_index[None, :] <= places[:, None])
        scores = (
            jnp.einsum("tjgd,njd->jgtn", queries, block_keys, preferred_element_type=jnp.float32)
            * score_scale
        )
        scores = jnp.where(allowed, scores, -1e30)
        new_max = jnp.maximum(run_max, jnp.max(scores, axis=-1))
        weights = jnp.exp(scores - new_max[..., None]) * allowed.astype(jnp.float32)
        new_sum = jnp.sum(weights, axis=-1)
        summed = jnp.einsum(
            "jgtn,njd->jgtd",
            weights.astype(jnp.bfloat16),
            block_values,
            preferred_element_type=jnp.float32,
        )
        return (new_max, new_sum, summed)

    touches = (
        (jnp.max(all_docs) >= query_low)
        & (jnp.min(all_docs) <= query_high)
        & (key_start <= query_last)
        & (key_start >= 0)
    )
    state = lax.cond(touches, accumulate, lambda inner: inner, initial)
    run_max, run_sum, run_acc = state
    result = run_acc / run_sum[..., None]
    attended = (
        jnp.transpose(result, (2, 0, 1, 3)).reshape(tok_rows, query_heads * HD).astype(jnp.bfloat16)
    )
    partial_value = jnp.dot(attended, w_out, preferred_element_type=jnp.float32)
    return lax.psum_scatter(
        partial_value.astype(jnp.bfloat16), "head", scatter_dimension=1, tiled=True
    )


def solution(mesh):
    return jax.shard_map(
        shards,
        mesh=mesh,
        in_specs=(
            P("ctx", None),
            P(None, "head"),
            P(None, "head"),
            P(None, "head"),
            P("head", None),
            P("ctx"),
        ),
        out_specs=P("ctx", "head"),
        check_vma=False,
    )
```

profile of v0, /device:TPU:0, one launch (start us, length us, event | category | flops | bytes accessed | tf_op | source)
XLA Modules:
  0.0 87.9 jit_solution(16131842945093330449)
XLA Ops:
  6.5 0.0 copy-start
  6.6 1.6 %copy-done = bf16[4096,256]{1,0:T(8,128)(2,1)S(1)} copy-done((bf16[4096,256]{1,0:T(8,128)(2,1)S(1)}, bf16[4096,256]{1,0:T(8,128)(2,1)}, u32[]{:S(2)}) %copy-start) | copy-done | bytes 2097176
  8.1 1.7 %convolution_convert_fusion.1 = bf16[128,256]{1,0:T(8,128)(2,1)S(1)} fusion(bf16[128,4096]{1,0:T(8,128)(2,1)} %param.8, bf16[4096,256]{1,0:T(8,128)(2,1)S(1)} %copy-done), kind=kOutput, calls=%fused_computation.15 | convolution fusion | flops 268468224 | bytes 3211264 | tf_op jit(solution)/shard_map/dot_general | solution.py:44
  9.8 2.4 %fusion.12 = f32[128,256]{1,0:T(8,128)S(1)} fusion(bf16[128,4096]{1,0:T(8,128)(2,1)} %param.8, bf16[4096,256]{1,0:T(8,128)(2,1)} %param.10), kind=kOutput, calls=%fused_computation.32 | convolution fusion | flops 268435456 | bytes 3276800 | tf_op jit(solution)/shard_map/dot_general | solution.py:41
  12.2 0.1 reshape.135
  12.3 0.3 multiply_cosine_fusion
  12.6 0.3 subtract_convert_fusion.1
  12.9 0.2 pad_maximum_fusion.2
  13.1 0.7 pad_maximum_fusion.1
  13.7 0.0 all-gather.3.cloned.1.call-update
  13.8 0.0 reduce-scatter.2.cloned.1.call-start
  13.8 10.3 %all-gather = s32[8,1,128]{2,1,0:T(1,128)S(1)} all-gather(s32[1,1,128]{2,1,0:T(1,128)S(1)} %bitcast.55), channel_id=1, replica_groups=mesh['ctx'=8,'head'=4] {'ctx'}, dimensions={0}, use_global_device_ids=true | all-gather | bytes 4608 | tf_op jit(solution)/shard_map/all_gather | solution.py:47
  24.1 0.7 fusion.10
  24.8 0.7 fusion.9
  28.1 4.6 %convolution_bitcast_fusion = f32[16,8,8,128]{3,1,2,0:T(8,128)S(1)} fusion(bf16[128,4096]{1,0:T(8,128)(2,1)S(1)} %copy-done.1, bf16[4096,1024]{1,0:T(8,128)(2,1)} %param.9), kind=kOutput, calls=%fused_computation.14 | convolution fusion | flops 1073741824 | bytes 9961472 | tf_op jit(solution)/shard_map/dot_general | solution.py:34
  32.7 0.1 copy.34
  32.8 0.3 subtract_convert_fusion
  33.2 0.1 pad_maximum_fusion
  33.3 6.7 %all-gather.3.cloned.1.call-done = bf16[1024,512]{1,0:T(8,128)(2,1)} async-done(((bf16[128,512]{1,0:T(8,128)(2,1)}), bf16[1024,512]{1,0:T(8,128)(2,1)}) %all-gather.3.cloned.1.call-update) | async-done | bytes 1048592 | tf_op jit(solution)/shard_map/all_gather | solution.py:57
  40.1 6.8 %conditional.1 = (f32[2,4,128]{2,1,0:T(4,128)S(1)}, f32[2,4,128,128]{2,3,1,0:T(8,128)}) conditional(s32[]{:T(128)} %convert_element_type.43, () %tuple.13, (s32[1024]{0:T(1024)S(1)}, s32[128]{0:T(128)S(1)}, s32[1024]{0:T(1024)S(1)}, s32[]{:T(128)}, s32[128]{0:T(128)S(1)}, /*index=5*/bf16[1024,512]{1,0:T(8,128)(2,1)}, ...), branch_computations={%region_4.0_spmd, %region_5.8_spmd} | conditional | flops 551025792 | bytes 22841392 | solution.py:90
  40.1 1.2 %compare_and_fusion = (pred[128,1024]{0,1:T(8,128)(4,1)S(1)}, f32[128,1024]{0,1:T(8,128)}) fusion(s32[128]{0:T(128)S(1)} %broadcast_add_fusion, s32[128]{0:T(128)S(1)} %get-tuple-element.22, s32[1024]{0:T(1024)S(1)} %get-tuple-element.23, s32[1024]{0:T(1024)S(1)} %get-tuple-element.21), kind=kLoop, calls=%fused_computation.7 | loop fusion | flops 524288 | bytes 664576 | tf_op jit(solution)/shard_map/cond/branch_1_fun/and | solution.py:67
  41.2 1.5 %copy.22 = bf16[1024,512]{0,1:T(8,128)(2,1)S(1)} copy(bf16[1024,512]{1,0:T(8,128)(2,1)} %get-tuple-element.44) | data formatting | bytes 2097152 | tf_op jit(solution)/shard_map
  42.7 0.0 copy-start.2
  42.7 0.1 fusion.11
  42.8 0.9 fusion
  43.7 0.1 copy-done.2
  43.8 2.1 %fusion.3 = f32[2,4,128,128]{2,3,1,0:T(8,128)} fusion(bf16[1024,2,128,1]{0,2,3,1:T(8,128)(2,1)S(1)} %bitcast.51, f32[2,1024,128,4]{2,1,3,0:T(8,128)S(1)} %get-tuple-element.56, f32[128,1024]{0,1:T(8,128)S(1)} %copy-done.2, f32[2,4,128]{2,1,0:T(4,128)S(1)} %broadcast_maximum_fusion, pred[128,1024]{0,1:T(8,128)(4,1)S(1)} %get-tuple-element.53), kind=kOutput, calls=%fused_computation.5 | convolution fusion | flops 273678336 | bytes 5902336 | tf_op jit(solution)/shard_map/cond | solution.py:90
  45.8 1.0 %fusion.2 = f32[2,4,128]{2,1,0:T(4,128)S(1)} fusion(f32[2,1024,128,4]{2,1,3,0:T(8,128)S(1)} %get-tuple-element.56, f32[128,1024]{0,1:T(8,128)S(1)} %copy-done.2, f32[2,4,128]{2,1,0:T(4,128)S(1)} %broadcast_maximum_fusion, pred[128,1024]{0,1:T(8,128)(4,1)S(1)} %get-tuple-element.53), kind=kLoop, calls=%fused_computation.4 | loop fusion | flops 5241856 | bytes 4857856 | tf_op jit(solution)/shard_map/cond/branch_1_fun/reduce_sum | solution.py:75
  46.9 1.1 %divide_convert_fusion = bf16[2,4,128,128]{2,3,1,0:T(8,128)(2,1)S(1)} fusion(f32[2,4,128,128]{2,3,1,0:T(8,128)} %get-tuple-element.46, f32[2,4,128]{2,1,0:T(4,128)S(1)} %get-tuple-element.31), kind=kLoop, calls=%fused_computation.16 | loop fusion | flops 262144 | bytes 790528 | tf_op jit(solution)/shard_map/convert_element_type | solution.py:94
  47.9 5.7 %convolution_convert_fusion = bf16[128,4096]{1,0:T(8,128)(2,1)} fusion(bf16[128,1024]{0,1:T(8,128)(2,1)S(1)} %bitcast.48, bf16[1024,4096]{1,0:T(8,128)(2,1)} %param.12), kind=kOutput, calls=%fused_computation.13 | convolution fusion | flops 1074266112 | bytes 9699328 | tf_op jit(solution)/shard_map/dot_general | solution.py:96
  53.6 0.0 reduce-scatter.2.cloned.1.call-update
  53.6 27.4 %reduce-scatter.2.cloned.1.call-done = bf16[128,1024]{1,0:T(8,128)(2,1)} async-done(((bf16[128,4096]{1,0:T(8,128)(2,1)}), bf16[128,1024]{1,0:T(8,128)(2,1)}) %reduce-scatter.2.cloned.1.call-update) | async-done | bytes 262160 | tf_op jit(solution)/shard_map/reduce_scatter | solution.py:97
  (14 shorter events, 0.1 us)
Async XLA Ops:
  6.5 1.6 %copy-start = (bf16[4096,256]{1,0:T(8,128)(2,1)S(1)}, bf16[4096,256]{1,0:T(8,128)(2,1)}, u32[]{:S(2)}) copy-start(bf16[4096,256]{1,0:T(8,128)(2,1)} %param.11) | copy-start | bytes 6291460
  6.5 21.5 %copy-start.1 = (bf16[128,4096]{1,0:T(8,128)(2,1)S(1)}, bf16[128,4096]{1,0:T(8,128)(2,1)}, u32[]{:S(2)}) copy-start(bf16[128,4096]{1,0:T(8,128)(2,1)} %param.8) | copy-start | bytes 3145732
  6.5 7.3 %copy-start.3 = (s32[128]{0:T(128)S(1)}, s32[128]{0:T(128)}, u32[]{:S(2)}) copy-start(s32[128]{0:T(128)} %param.13) | copy-start | bytes 1540
  6.5 33.5 %all-gather.3.cloned.1.call-start = ((), (), s32[]{:S(2)}) async-start(), calls=%async_computation.1 | async-start | bytes 1179648 | tf_op jit(solution)/shard_map/all_gather | solution.py:57
  13.8 67.3 %reduce-scatter.2.cloned.1.call-start = ((), (), s32[]{:S(2)}) async-start(), calls=%async_computation.2 | async-start | bytes 1310720 | tf_op jit(solution)/shard_map/reduce_scatter | solution.py:97
  42.7 1.0 %copy-start.2 = (f32[128,1024]{0,1:T(8,128)S(1)}, f32[128,1024]{0,1:T(8,128)}, u32[]{:S(2)}) copy-start(f32[128,1024]{0,1:T(8,128)} %get-tuple-element.54) | copy-start | bytes 1572868 | tf_op jit(solution)/shard_map/cond
Sparse Core Ops, SparseCore 0:
  13.9 26.1 all-gather.2
  53.8 27.2 reduce-scatter.1
where the time goes:
time: 88.3 us; the launch traced here: 87.9 us
  waiting for transfers between devices  34.2 us (39%)
  matrix products  17.3 us (20%)
  between operations  16.1 us (18%)
  blocking collectives  10.3 us (12%)
  other arithmetic  6.54 us (7%)
  local copies, waits for them, and re-layouts  3.45 us (4%)
    reduce_scatter x1, waiting for transfers between devices, shards(): lax.psum_scatter(partial_value.astype(jnp.bfloat16), 'head', scatter_dime...  27.4 us
    all_gather x1, blocking collectives, shards(): all_docs = lax.all_gather(doc_ids, 'ctx', axis=0, tiled=True)  10.3 us
    all_gather x1, waiting for transfers between devices, shards(): block_kv = lax.all_gather(packed, 'ctx', axis=0, tiled=True)  6.74 us
    dot_general x1, matrix products, shards(): partial_value = jnp.dot(attended, w_out, preferred_element_type=jnp.float32)  5.67 us
    dot_general x1, matrix products, shards(): jnp.dot(tokens, w_query, preferred_element_type=jnp.float32)  4.63 us
    dot_general x1, matrix products, shards(): jnp.dot(tokens, w_key, preferred_element_type=jnp.float32)  2.36 us
    cond x1, matrix products, shards(): state = lax.cond(touches, accumulate, lambda inner: inner, initial)  2.09 us
  transfers between devices with their start and end apart: 2, of which 2 were waited for; matrix products, arithmetic and copies ran while one was open for 8% of the time, Pallas kernels for 0%

commit v1 on v0

v1 whole, which is shorter than its diff:
```python
import functools
import math

import jax
import jax.numpy as jnp
import numpy as np
from jax import lax
from jax.experimental import pallas as pl
from jax.experimental.pallas import tpu as pltpu
from jax.sharding import PartitionSpec as P

HD = 128
STEPS = 4
SUB = 2
MESH = pl.DeviceIdType.MESH


def kernel(
    n_ctx, n_head,
    tokens, w_query, w_key, w_value, w_out, docs, freqs, out,
    tok, wq, wk, wv, wo, freq, doc_all, kv, q_acc, kv_acc, q, cos_ref, sin_ref, doc_q,
    sc, top, tot, acc, att, part, rbuf,
    tok_sem, wq_sem, wk_sem, wv_sem, wo_sem, small_sem,
    kv_send, kv_fwd, kv_recv, part_send, part_recv,
):
    rows = tokens.shape[0]
    kv_heads = w_key.shape[1] // HD
    heads = w_query.shape[1] // HD
    group = heads // kv_heads
    kv_width = kv_heads * HD
    chips = n_ctx // 2
    me = lax.axis_index("ctx")
    z = lax.axis_index("head")
    core = lax.rem(me, 2)
    chip = me // 2
    partner = me + 1 - 2 * core
    step_rows = wq.shape[1]
    piece = wo.shape[2]

    def tok_copy(c):
        return pltpu.make_async_copy(
            tokens.at[:, pl.ds(pl.multiple_of(c * step_rows, step_rows), step_rows)],
            tok.at[c], tok_sem.at[c])

    def rows_copy(src, dst, sem, c):
        return pltpu.make_async_copy(
            src.at[pl.ds(pl.multiple_of(c * step_rows, step_rows), step_rows), :],
            dst.at[c], sem.at[c])

    def wo_copy(p):
        return pltpu.make_async_copy(
            w_out.at[:, pl.ds(pl.multiple_of(p * piece, piece), piece)], wo.at[p], wo_sem.at[p])

    doc_copy = pltpu.make_async_copy(docs, doc_all.at[me], small_sem.at[0])
    freq_copy = pltpu.make_async_copy(freqs, freq, small_sem.at[1])

    def piece_of(k):
        return jnp.where(z < n_head // 2, n_head * SUB - 1 - k, k)

    doc_copy.start()
    freq_copy.start()
    for c in range(STEPS):
        tok_copy(c).start()
        rows_copy(w_key, wk, wk_sem, c).start()
        rows_copy(w_value, wv, wv_sem, c).start()
    rows_copy(w_query, wq, wq_sem, 0).start()

    barrier = pltpu.get_barrier_semaphore()

    def greet(c, carry):
        @pl.when(c != chip)
        def _():
            pl.semaphore_signal(
                barrier, inc=1, device_id={"ctx": c * 2 + core}, device_id_type=MESH)
        return carry

    lax.fori_loop(0, chips, greet, 0)
    pl.semaphore_signal(barrier, inc=1, device_id={"ctx": partner}, device_id_type=MESH)

    @pl.when(z > 0)
    def _():
        pl.semaphore_signal(barrier, inc=1, device_id={"head": z - 1}, device_id_type=MESH)

    @pl.when(z < n_head - 1)
    def _():
        pl.semaphore_signal(barrier, inc=1, device_id={"head": z + 1}, device_id_type=MESH)

    freq_copy.wait()
    doc_copy.wait()
    places = (me * rows + lax.broadcasted_iota(jnp.int32, (rows, HD), 0)).astype(jnp.float32)
    angles = places * freq[...]
    lane = lax.broadcasted_iota(jnp.int32, (rows, HD), 1)
    cos_ref[...] = jnp.cos(angles)
    sine = jnp.sin(angles)
    sin_ref[...] = jnp.where(lane < HD // 2, -sine, sine)
    doc_q[...] = jnp.broadcast_to(doc_all[me].astype(jnp.float32), (rows, rows)).T

    def rotated(x):
        return (x * cos_ref[...] + pltpu.roll(x, HD // 2, 1) * sin_ref[...]).astype(jnp.bfloat16)

    kv_acc[...] = jnp.zeros_like(kv_acc)

    def kv_step(c, carry):
        tok_copy(c).wait()
        rows_copy(w_key, wk, wk_sem, c).wait()
        rows_copy(w_value, wv, wv_sem, c).wait()

        @pl.when(c > 0)
        def _():
            rows_copy(w_query, wq, wq_sem, c).start()
        kv_acc[:, :kv_width] += jnp.dot(tok[c], wk[c], preferred_element_type=jnp.float32)
        kv_acc[:, kv_width:] += jnp.dot(tok[c], wv[c], preferred_element_type=jnp.float32)
        return carry

    lax.fori_loop(0, STEPS, kv_step, 0)
    for h in range(kv_heads):
        kv[me, :, h * HD:(h + 1) * HD] = rotated(kv_acc[:, h * HD:(h + 1) * HD])
    kv[me, :, kv_width:] = kv_acc[:, kv_width:].astype(jnp.bfloat16)

    pl.semaphore_wait(
        barrier,
        chips + (z > 0).astype(jnp.int32) + (z < n_head - 1).astype(jnp.int32))

    def block_copies(block, sems, slot, target):
        return [
            pltpu.make_async_remote_copy(
                src_ref=ref.at[block], dst_ref=ref.at[block],
                send_sem=sems.at[i, slot], recv_sem=kv_recv.at[i, block],
                device_id={"ctx": target}, device_id_type=MESH)
            for i, ref in enumerate((kv, doc_all))
        ]

    def send_one(i, carry):
        c = chips - 1 - i
        for copy in block_copies(me, kv_send, c, c * 2 + core):
            copy.start()
        return carry

    lax.fori_loop(0, chips - 1 - chip, send_one, 0)

    @pl.when(core == 0)
    def _():
        for copy in block_copies(me, kv_send, chip, partner):
            copy.start()

    q_acc[...] = jnp.zeros_like(q_acc)

    def q_step(c, carry):
        rows_copy(w_query, wq, wq_sem, c).wait()
        for i in range(n_head * SUB // STEPS):
            wo_copy(piece_of(c * (n_head * SUB // STEPS) + i)).start()
        q_acc[...] += jnp.dot(tok[c], wq[c], preferred_element_type=jnp.float32)
        return carry

    lax.fori_loop(0, STEPS, q_step, 0)
    for h in range(heads):
        q[h] = rotated(q_acc[:, h * HD:(h + 1) * HD])

    def score_block(j, own):
        ok = doc_q[...] == doc_all[j].astype(jnp.float32)
        if own:
            ok = ok & (lane <= lax.broadcasted_iota(jnp.int32, (rows, rows), 0))
        bias = jnp.where(ok, 0.0, -1e30).astype(jnp.float32)
        for h in range(kv_heads):
            s = lax.dot_general(
                q[h * group:(h + 1) * group].reshape(group * rows, HD),
                kv[j, :, h * HD:(h + 1) * HD],
                (((1,), (1,)), ((), ())), preferred_element_type=jnp.float32)
            s = (s.reshape(group, rows, rows) + bias[None]).reshape(group * rows, rows)
            sc[j, h] = s
            top[h] = s if own else jnp.maximum(top[h], s)

    score_block(me, True)

    def wait_block(j):
        for copy in block_copies(j, kv_fwd, 0, partner):
            copy.wait_recv()

    @pl.when(core == 1)
    def _():
        wait_block(me - 1)
        score_block(me - 1, False)

    def chip_step(i, carry):
        s = chip - 1 - i
        mine = s * 2 + core
        wait_block(mine)
        for copy in block_copies(mine, kv_fwd, s, partner):
            copy.start()
        score_block(mine, False)
        other = s * 2 + 1 - core
        wait_block(other)
        score_block(other, False)
        return carry

    lax.fori_loop(0, chip, chip_step, 0)

    factor = math.log2(math.e) / math.sqrt(HD)
    for h in range(kv_heads):
        top[h] = jnp.broadcast_to(jnp.max(top[h], axis=1, keepdims=True), top.shape[1:])
    tot[...] = jnp.zeros_like(tot)
    acc[...] = jnp.zeros_like(acc)

    def weigh(j, carry):
        for h in range(kv_heads):
            p = jnp.exp2((sc[j, h] - top[h]) * factor)
            tot[h] += p
            acc[h] += jnp.dot(
                p.astype(jnp.bfloat16), kv[j, :, kv_width + h * HD:kv_width + (h + 1) * HD],
                preferred_element_type=jnp.float32)
        return carry

    lax.fori_loop(0, me + 1, weigh, 0)
    for h in range(kv_heads):
        result = (acc[h] / jnp.sum(tot[h], axis=1, keepdims=True)).astype(jnp.bfloat16)
        for g in range(group):
            att[:, (h * group + g) * HD:(h * group + g + 1) * HD] = result[g * rows:(g + 1) * rows]

    def piece_copy(p, way):
        target = z + 1 if way == 0 else z - 1
        return pltpu.make_async_remote_copy(
            src_ref=part.at[p], dst_ref=rbuf.at[way, p],
            send_sem=part_send.at[p], recv_sem=part_recv.at[way, p],
            device_id={"head": target}, device_id_type=MESH)

    def project(k, carry):
        p = piece_of(k)
        wo_copy(p).wait()
        part[p] = jnp.dot(att[...], wo[p], preferred_element_type=jnp.float32).astype(jnp.bfloat16)

        @pl.when((z == 0) & (p >= SUB))
        def _():
            piece_copy(p, 0).start()

        @pl.when((z == n_head - 1) & (p < (n_head - 1) * SUB))
        def _():
            piece_copy(p, 1).start()
        return carry

    lax.fori_loop(0, n_head * SUB, project, 0)

    def pass_on(p, way):
        piece_copy(p, way).wait_recv()
        part[p] = (part[p].astype(jnp.float32) + rbuf[way, p].astype(jnp.float32)).astype(jnp.bfloat16)
        piece_copy(p, way).start()

    def relay(t, carry):
        a = t - z
        b = t - (n_head - 1 - z)

        @pl.when((z > 0) & (a >= 0) & (a < SUB * (n_head - 1 - z)))
        def _():
            pass_on(n_head * SUB - 1 - a, 0)

        @pl.when((z < n_head - 1) & (b >= 0) & (b < SUB * z))
        def _():
            pass_on(b, 1)
        return carry

    @pl.when((z > 0) & (z < n_head - 1))
    def _():
        lax.fori_loop(0, SUB * (n_head - 1) + n_head, relay, 0)

    def last(s, add_left, add_right):
        p = z * SUB + s
        value = part[p].astype(jnp.float32)
        if add_left:
            piece_copy(p, 0).wait_recv()
            value += rbuf[0, p].astype(jnp.float32)
        if add_right:
            piece_copy(p, 1).wait_recv()
            value += rbuf[1, p].astype(jnp.float32)
        out[:, s * piece:(s + 1) * piece] = value.astype(jnp.bfloat16)

    for which, left, right in ((z == 0, False, True), (z == n_head - 1, True, False),
                               ((z > 0) & (z < n_head - 1), True, True)):
        @pl.when(which)
        def _(left=left, right=right):
            for s in reversed(range(SUB)) if left else range(SUB):
                last(s, left, right)

    def drain_one(c, carry):
        for copy in block_copies(me, kv_send, c, c * 2 + core):
            copy.wait_send()
        return carry

    lax.fori_loop(chip + 1, chips, drain_one, 0)

    @pl.when(core == 0)
    def _():
        for copy in block_copies(me, kv_send, chip, partner):
            copy.wait_send()

    def drain_forward(s, carry):
        for copy in block_copies(s * 2 + core, kv_fwd, s, partner):
            copy.wait_send()
        return carry

    lax.fori_loop(0, chip, drain_forward, 0)

    def drain_piece(p, carry):
        @pl.when((p < z * SUB) | (p >= (z + 1) * SUB))
        def _():
            piece_copy(p, 0).wait_send()
        return carry

    lax.fori_loop(0, n_head * SUB, drain_piece, 0)


def solution(mesh):
    n_ctx, n_head = mesh.shape["ctx"], mesh.shape["head"]
    half = HD // 2
    base = 500000.0 ** (-2.0 * np.arange(half, dtype=np.float64) / HD)
    table = np.concatenate([base, base]).astype(np.float32)[None, :]

    def step(tokens, w_query, w_key, w_value, w_out, doc_ids):
        rows, width = tokens.shape
        q_width, kv_width = w_query.shape[1], w_key.shape[1]
        kv_heads, heads = kv_width // HD, q_width // HD
        group = heads // kv_heads
        step_rows = width // STEPS
        out_width = w_out.shape[1]
        pieces = n_head * SUB
        piece = out_width // pieces
        bf16, f32 = jnp.bfloat16, jnp.float32
        dma = pltpu.SemaphoreType.DMA
        return pl.pallas_call(
            functools.partial(kernel, n_ctx, n_head),
            out_shape=jax.ShapeDtypeStruct((rows, out_width // n_head), bf16),
            in_specs=[pl.BlockSpec(memory_space=pl.ANY)] * 7,
            out_specs=pl.BlockSpec(memory_space=pltpu.VMEM),
            scratch_shapes=[
                pltpu.VMEM((STEPS, rows, step_rows), bf16),
                pltpu.VMEM((STEPS, step_rows, q_width), bf16),
                pltpu.VMEM((STEPS, step_rows, kv_width), bf16),
                pltpu.VMEM((STEPS, step_rows, kv_width), bf16),
                pltpu.VMEM((pieces, q_width, piece), bf16),
                pltpu.VMEM((1, HD), f32),
                pltpu.VMEM((n_ctx, 1, rows), jnp.int32),
                pltpu.VMEM((n_ctx, rows, 2 * kv_width), bf16),
                pltpu.VMEM((rows, q_width), f32),
                pltpu.VMEM((rows, 2 * kv_width), f32),
                pltpu.VMEM((heads, rows, HD), bf16),
                pltpu.VMEM((rows, HD), f32),
                pltpu.VMEM((rows, HD), f32),
                pltpu.VMEM((rows, rows), f32),
                pltpu.VMEM((n_ctx, kv_heads, group * rows, rows), f32),
                pltpu.VMEM((kv_heads, group * rows, rows), f32),
                pltpu.VMEM((kv_heads, group * rows, rows), f32),
                pltpu.VMEM((kv_heads, group * rows, HD), f32),
                pltpu.VMEM((rows, q_width), bf16),
                pltpu.VMEM((pieces, rows, piece), bf16),
                pltpu.VMEM((2, pieces, rows, piece), bf16),
                dma((STEPS,)), dma((STEPS,)), dma((STEPS,)), dma((STEPS,)), dma((pieces,)), dma((2,)),
                dma((2, n_ctx // 2)), dma((2, n_ctx // 2)), dma((2, n_ctx)),
                dma((pieces,)), dma((2, pieces)),
            ],
            compiler_params=pltpu.CompilerParams(
                collective_id=0, has_side_effects=True, vmem_limit_bytes=60 * 1024 * 1024),
            name="attention_layer",
        )(tokens, w_query, w_key, w_value, w_out, doc_ids.reshape(1, rows), jnp.asarray(table))

    return jax.shard_map(
        step,
        mesh=mesh,
        in_specs=(
            P("ctx", None),
            P(None, "head"),
            P(None, "head"),
            P(None, "head"),
            P("head", None),
            P("ctx"),
        ),
        out_specs=P("ctx", "head"),
        check_vma=False,
    )
```

time: 88.3 us -> 38.5 us (0.44)
  the two profiles are of different devices: /device:TPU:0 before, /device:TPU:22 now
where the time goes in v1:
time: 38.5 us; the launch traced here: 38.4 us
  Pallas kernels  36.7 us (95%)
  local copies, waits for them, and re-layouts  1.67 us (4%)
    pallas_call x1, Pallas kernels, step(): pl.pallas_call(functools.partial(kernel, n_ctx, n_head), out_shape=jax.Sh...  36.7 us
    unnamed x1, local copies, waits for them, and re-layouts  1.67 us

profile of v1, /device:TPU:22, one launch (start us, length us, event | category | flops | bytes accessed | tf_op | source)
XLA Modules:
  0.0 38.4 jit_solution(10591884421511544220)
XLA Ops:
  0.0 36.7 %attention_layer.1 = bf16[128,1024]{1,0:T(8,128)(2,1)} custom-call(bf16[128,4096]{1,0:T(8,128)(2,1)} %tokens.1, bf16[4096,1024]{1,0:T(8,128)(2,1)} %w_query.1, bf16[4096,256]{1,0:T(8,128)(2,1)} %w_key.1, bf16[4096,256]{1,0:T(8,128)(2,1)} %w_value.1, bf16[1024,4096]{1,0:T(8,128)(2,1)} %w_out.1, s32[1,128]{1,0:T(1,128)} %bitcast.1, f32[1,128]{1,0:T(1,128)} %constant.2.clone.freqs), custom_call_target="tpu_custom_call" | custom-call | tf_op jit(solution)/shard_map/attention_layer/pallas_call | solution.py:327
  36.7 1.7 %copy.9 = bf16[128,1024]{1,0:T(8,128)(2,1)} copy(bf16[128,1024]{1,0:T(8,128)(2,1)} %attention_layer.1) | data formatting | bytes 524288

commit v2 on v1

v2 whole, which is shorter than its diff:
```python
import functools
import math

import jax
import jax.numpy as jnp
import numpy as np
from jax import lax
from jax.experimental import pallas as pl
from jax.experimental.pallas import tpu as pltpu
from jax.sharding import PartitionSpec as P

HD = 128
STEPS = 4
SUB = 2
PARTS = 2
MESH = pl.DeviceIdType.MESH


def kernel(
    n_ctx, n_head,
    tokens, w_query, w_key, w_value, w_out, docs, freqs, out,
    tok, wq, wk, wv, wo, freq, doc_all, keys, values, q_acc, k_acc, v_acc, q, cos_ref, sin_ref, doc_q,
    sc, top, tot, acc, att, part, rbuf,
    tok_sem, wq_sem, wk_sem, wv_sem, wo_sem, small_sem,
    kv_send, kv_fwd, kv_recv, part_send, part_recv,
):
    rows = tokens.shape[0]
    kv_heads = w_key.shape[1] // HD
    heads = w_query.shape[1] // HD
    group = heads // kv_heads
    part_rows = rows // PARTS
    chips = n_ctx // 2
    me = lax.axis_index("ctx")
    z = lax.axis_index("head")
    core = lax.rem(me, 2)
    chip = me // 2
    partner = me + 1 - 2 * core
    step_rows = wq.shape[1]
    piece = wo.shape[2]

    def tok_copy(c):
        return pltpu.make_async_copy(
            tokens.at[:, pl.ds(pl.multiple_of(c * step_rows, step_rows), step_rows)],
            tok.at[c], tok_sem.at[c])

    def rows_copy(src, dst, sem, c):
        return pltpu.make_async_copy(
            src.at[pl.ds(pl.multiple_of(c * step_rows, step_rows), step_rows), :],
            dst.at[c], sem.at[c])

    def wo_copy(p):
        return pltpu.make_async_copy(
            w_out.at[:, pl.ds(pl.multiple_of(p * piece, piece), piece)], wo.at[p], wo_sem.at[p])

    doc_copy = pltpu.make_async_copy(docs, doc_all.at[me], small_sem.at[0])
    freq_copy = pltpu.make_async_copy(freqs, freq, small_sem.at[1])

    def piece_of(k):
        return jnp.where(z < n_head // 2, n_head * SUB - 1 - k, k)

    doc_copy.start()
    freq_copy.start()
    for c in range(STEPS):
        tok_copy(c).start()
        rows_copy(w_key, wk, wk_sem, c).start()
    for c in range(STEPS):
        rows_copy(w_value, wv, wv_sem, c).start()

    barrier = pltpu.get_barrier_semaphore()

    def greet(c, carry):
        @pl.when(c != chip)
        def _():
            pl.semaphore_signal(
                barrier, inc=1, device_id={"ctx": c * 2 + core}, device_id_type=MESH)
        return carry

    lax.fori_loop(0, chips, greet, 0)
    pl.semaphore_signal(barrier, inc=1, device_id={"ctx": partner}, device_id_type=MESH)

    @pl.when(z > 0)
    def _():
        pl.semaphore_signal(barrier, inc=1, device_id={"head": z - 1}, device_id_type=MESH)

    @pl.when(z < n_head - 1)
    def _():
        pl.semaphore_signal(barrier, inc=1, device_id={"head": z + 1}, device_id_type=MESH)

    freq_copy.wait()
    doc_copy.wait()
    places = (me * rows + lax.broadcasted_iota(jnp.int32, (rows, HD), 0)).astype(jnp.float32)
    angles = places * freq[...]
    lane = lax.broadcasted_iota(jnp.int32, (rows, HD), 1)
    cos_ref[...] = jnp.cos(angles)
    sine = jnp.sin(angles)
    sin_ref[...] = jnp.where(lane < HD // 2, -sine, sine)
    doc_q[...] = jnp.broadcast_to(doc_all[me].astype(jnp.float32), (rows, rows)).T

    def rotated(x):
        return (x * cos_ref[...] + pltpu.roll(x, HD // 2, 1) * sin_ref[...]).astype(jnp.bfloat16)

    def copies(refs, block, sems, slot, target):
        return [
            pltpu.make_async_remote_copy(
                src_ref=ref.at[block], dst_ref=ref.at[block],
                send_sem=sems.at[i, slot], recv_sem=kv_recv.at[i, block],
                device_id={"ctx": target}, device_id_type=MESH)
            for i, ref in refs
        ]

    first, second = ((0, keys), (1, doc_all)), ((2, values),)

    def send_all(refs):
        def send_one(i, carry):
            c = chips - 1 - i
            for copy in copies(refs, me, kv_send, c, c * 2 + core):
                copy.start()
            return carry

        lax.fori_loop(0, chips - 1 - chip, send_one, 0)

        @pl.when(core == 0)
        def _():
            for copy in copies(refs, me, kv_send, chip, partner):
                copy.start()

    k_acc[...] = jnp.zeros_like(k_acc)

    def key_step(c, carry):
        tok_copy(c).wait()
        rows_copy(w_key, wk, wk_sem, c).wait()
        k_acc[...] += jnp.dot(tok[c], wk[c], preferred_element_type=jnp.float32)
        return carry

    lax.fori_loop(0, STEPS, key_step, 0)
    for h in range(kv_heads):
        keys[me, :, h * HD:(h + 1) * HD] = rotated(k_acc[:, h * HD:(h + 1) * HD])
    pl.semaphore_wait(
        barrier,
        chips + (z > 0).astype(jnp.int32) + (z < n_head - 1).astype(jnp.int32))
    send_all(first)

    v_acc[...] = jnp.zeros_like(v_acc)

    def value_step(c, carry):
        rows_copy(w_value, wv, wv_sem, c).wait()
        rows_copy(w_query, wq, wq_sem, c).start()
        v_acc[...] += jnp.dot(tok[c], wv[c], preferred_element_type=jnp.float32)
        return carry

    lax.fori_loop(0, STEPS, value_step, 0)
    values[me] = v_acc[...].astype(jnp.bfloat16)
    send_all(second)

    q_acc[...] = jnp.zeros_like(q_acc)

    def q_step(c, carry):
        rows_copy(w_query, wq, wq_sem, c).wait()
        for i in range(n_head * SUB // STEPS):
            wo_copy(piece_of(c * (n_head * SUB // STEPS) + i)).start()
        q_acc[...] += jnp.dot(tok[c], wq[c], preferred_element_type=jnp.float32)
        return carry

    lax.fori_loop(0, STEPS, q_step, 0)
    for h in range(heads):
        turned = rotated(q_acc[:, h * HD:(h + 1) * HD])
        for r in range(PARTS):
            q[h // group, r, h % group] = turned[r * part_rows:(r + 1) * part_rows]

    def score_block(j, own):
        ok = doc_q[...] == doc_all[j].astype(jnp.float32)
        if own:
            ok = ok & (lane <= lax.broadcasted_iota(jnp.int32, (rows, rows), 0))
        bias = jnp.where(ok, 0.0, -1e30).astype(jnp.float32)
        for h in range(kv_heads):
            s = lax.dot_general(
                q[h].reshape(group * rows, HD), keys[j, :, h * HD:(h + 1) * HD],
                (((1,), (1,)), ((), ())), preferred_element_type=jnp.float32)
            s = s.reshape(PARTS, group, part_rows, rows) + bias.reshape(PARTS, 1, part_rows, rows)
            s = s.reshape(PARTS, group * part_rows, rows)
            sc[j, h] = s
            top[h] = s if own else jnp.maximum(top[h], s)

    score_block(me, True)

    def wait_block(refs, j):
        for copy in copies(refs, j, kv_fwd, 0, partner):
            copy.wait_recv()

    def receive(refs, use):
        @pl.when(core == 1)
        def _():
            wait_block(refs, me - 1)
            use(me - 1)

        def chip_step(i, carry):
            s = chip - 1 - i
            mine = s * 2 + core
            wait_block(refs, mine)
            for copy in copies(refs, mine, kv_fwd, s, partner):
                copy.start()
            use(mine)
            other = s * 2 + 1 - core
            wait_block(refs, other)
            use(other)
            return carry

        lax.fori_loop(0, chip, chip_step, 0)

    receive(first, lambda j: score_block(j, False))
    receive(second, lambda j: None)

    factor = math.log2(math.e) / math.sqrt(HD)
    def attend(r):
        for h in range(kv_heads):
            top[h, r] = jnp.broadcast_to(
                jnp.max(top[h, r], axis=1, keepdims=True), top.shape[2:])
            tot[h] = jnp.zeros(tot.shape[1:], jnp.float32)
            acc[h] = jnp.zeros(acc.shape[1:], jnp.float32)

        def weigh(j, carry):
            for h in range(kv_heads):
                p = jnp.exp2((sc[j, h, r] - top[h, r]) * factor)
                tot[h] += p
                acc[h] += jnp.dot(
                    p.astype(jnp.bfloat16), values[j, :, h * HD:(h + 1) * HD],
                    preferred_element_type=jnp.float32)
            return carry

        lax.fori_loop(0, me + 1, weigh, 0)
        for h in range(kv_heads):
            result = (acc[h] / jnp.sum(tot[h], axis=1, keepdims=True)).astype(jnp.bfloat16)
            for g in range(group):
                att[r, :, (h * group + g) * HD:(h * group + g + 1) * HD] = (
                    result[g * part_rows:(g + 1) * part_rows])

    def piece_copy(r, p, way):
        target = z + 1 if way == 0 else z - 1
        return pltpu.make_async_remote_copy(
            src_ref=part.at[r, p], dst_ref=rbuf.at[way, r, p],
            send_sem=part_send.at[r, p], recv_sem=part_recv.at[way, r, p],
            device_id={"head": target}, device_id_type=MESH)

    def both(r, whole):
        attend(r)

        def project(k, carry):
            p = piece_of(k)

            @pl.when(r == 0)
            def _():
                wo_copy(p).wait()
            part[r, p] = jnp.dot(
                att[r], wo[p], preferred_element_type=jnp.float32).astype(jnp.bfloat16)

            @pl.when((z == 0) & (p >= SUB))
            def _():
                piece_copy(r, p, 0).start()

            @pl.when((z == n_head - 1) & (p < (n_head - 1) * SUB))
            def _():
                piece_copy(r, p, 1).start()
            return carry

        lax.fori_loop(0, n_head * SUB, project, 0)
        return whole

    lax.fori_loop(0, PARTS, both, 0)

    def pass_on(r, p, way):
        piece_copy(r, p, way).wait_recv()
        part[r, p] = (
            part[r, p].astype(jnp.float32) + rbuf[way, r, p].astype(jnp.float32)
        ).astype(jnp.bfloat16)
        piece_copy(r, p, way).start()

    def relay(r, t):
        a = t - z
        b = t - (n_head - 1 - z)

        @pl.when((z > 0) & (a >= 0) & (a < SUB * (n_head - 1 - z)))
        def _():
            pass_on(r, n_head * SUB - 1 - a, 0)

        @pl.when((z < n_head - 1) & (b >= 0) & (b < SUB * z))
        def _():
            pass_on(r, b, 1)

    length = SUB * (n_head - 1) + n_head

    def relay_step(i, carry):
        relay(i // length, lax.rem(i, length))
        return carry

    @pl.when((z > 0) & (z < n_head - 1))
    def _():
        lax.fori_loop(0, PARTS * length, relay_step, 0)

    def last(r, s, add_left, add_right):
        p = z * SUB + s
        value = part[r, p].astype(jnp.float32)
        if add_left:
            piece_copy(r, p, 0).wait_recv()
            value += rbuf[0, r, p].astype(jnp.float32)
        if add_right:
            piece_copy(r, p, 1).wait_recv()
            value += rbuf[1, r, p].astype(jnp.float32)
        out[r * part_rows:(r + 1) * part_rows, s * piece:(s + 1) * piece] = (
            value.astype(jnp.bfloat16))

    for which, left, right in ((z == 0, False, True), (z == n_head - 1, True, False),
                               ((z > 0) & (z < n_head - 1), True, True)):
        @pl.when(which)
        def _(left=left, right=right):
            for r in range(PARTS):
                for s in reversed(range(SUB)) if left else range(SUB):
                    last(r, s, left, right)

    everything = first + second

    def drain_one(c, carry):
        for copy in copies(everything, me, kv_send, c, c * 2 + core):
            copy.wait_send()
        return carry

    lax.fori_loop(chip + 1, chips, drain_one, 0)

    @pl.when(core == 0)
    def _():
        for copy in copies(everything, me, kv_send, chip, partner):
            copy.wait_send()

    def drain_forward(s, carry):
        for copy in copies(everything, s * 2 + core, kv_fwd, s, partner):
            copy.wait_send()
        return carry

    lax.fori_loop(0, chip, drain_forward, 0)

    def drain_piece(p, carry):
        @pl.when((p < z * SUB) | (p >= (z + 1) * SUB))
        def _():
            for r in range(PARTS):
                piece_copy(r, p, 0).wait_send()
        return carry

    lax.fori_loop(0, n_head * SUB, drain_piece, 0)


def solution(mesh):
    n_ctx, n_head = mesh.shape["ctx"], mesh.shape["head"]
    half = HD // 2
    base = 500000.0 ** (-2.0 * np.arange(half, dtype=np.float64) / HD)
    table = np.concatenate([base, base]).astype(np.float32)[None, :]

    def step(tokens, w_query, w_key, w_value, w_out, doc_ids):
        rows, width = tokens.shape
        q_width, kv_width = w_query.shape[1], w_key.shape[1]
        kv_heads, heads = kv_width // HD, q_width // HD
        group = heads // kv_heads
        step_rows = width // STEPS
        part_rows = rows // PARTS
        out_width = w_out.shape[1]
        pieces = n_head * SUB
        piece = out_width // pieces
        bf16, f32 = jnp.bfloat16, jnp.float32
        dma = pltpu.SemaphoreType.DMA
        return pl.pallas_call(
            functools.partial(kernel, n_ctx, n_head),
            out_shape=jax.ShapeDtypeStruct((rows, out_width // n_head), bf16),
            in_specs=[pl.BlockSpec(memory_space=pl.ANY)] * 7,
            out_specs=pl.BlockSpec(memory_space=pltpu.VMEM),
            scratch_shapes=[
                pltpu.VMEM((STEPS, rows, step_rows), bf16),
                pltpu.VMEM((STEPS, step_rows, q_width), bf16),
                pltpu.VMEM((STEPS, step_rows, kv_width), bf16),
                pltpu.VMEM((STEPS, step_rows, kv_width), bf16),
                pltpu.VMEM((pieces, q_width, piece), bf16),
                pltpu.VMEM((1, HD), f32),
                pltpu.VMEM((n_ctx, 1, rows), jnp.int32),
                pltpu.VMEM((n_ctx, rows, kv_width), bf16),
                pltpu.VMEM((n_ctx, rows, kv_width), bf16),
                pltpu.VMEM((rows, q_width), f32),
                pltpu.VMEM((rows, kv_width), f32),
                pltpu.VMEM((rows, kv_width), f32),
                pltpu.VMEM((kv_heads, PARTS, group, rows // PARTS, HD), bf16),
                pltpu.VMEM((rows, HD), f32),
                pltpu.VMEM((rows, HD), f32),
                pltpu.VMEM((rows, rows), f32),
                pltpu.VMEM((n_ctx, kv_heads, PARTS, group * part_rows, rows), f32),
                pltpu.VMEM((kv_heads, PARTS, group * part_rows, rows), f32),
                pltpu.VMEM((kv_heads, group * part_rows, rows), f32),
                pltpu.VMEM((kv_heads, group * part_rows, HD), f32),
                pltpu.VMEM((PARTS, part_rows, q_width), bf16),
                pltpu.VMEM((PARTS, pieces, part_rows, piece), bf16),
                pltpu.VMEM((2, PARTS, pieces, part_rows, piece), bf16),
                dma((STEPS,)), dma((STEPS,)), dma((STEPS,)), dma((STEPS,)), dma((pieces,)), dma((2,)),
                dma((3, n_ctx // 2)), dma((3, n_ctx // 2)), dma((3, n_ctx)),
                dma((PARTS, pieces)), dma((2, PARTS, pieces)),
            ],
            compiler_params=pltpu.CompilerParams(
                collective_id=0, has_side_effects=True, vmem_limit_bytes=60 * 1024 * 1024),
            name="attention_layer",
        )(tokens, w_query, w_key, w_value, w_out, doc_ids.reshape(1, rows), jnp.asarray(table))

    return jax.shard_map(
        step,
        mesh=mesh,
        in_specs=(
            P("ctx", None),
            P(None, "head"),
            P(None, "head"),
            P(None, "head"),
            P("head", None),
            P("ctx"),
        ),
        out_specs=P("ctx", "head"),
        check_vma=False,
    )
```

time: 38.5 us -> 45.5 us (1.18)
  the two profiles are of different devices: /device:TPU:22 before, /device:TPU:6 now
where the time goes in v2:
time: 45.5 us; the launch traced here: 45.4 us
  Pallas kernels  43.7 us (96%)
  local copies, waits for them, and re-layouts  1.67 us (4%)
    pallas_call x1, Pallas kernels, step(): pl.pallas_call(functools.partial(kernel, n_ctx, n_head), out_shape=jax.Sh...  43.7 us
    unnamed x1, local copies, waits for them, and re-layouts  1.67 us

profile of v2, /device:TPU:6, one launch (start us, length us, event | category | flops | bytes accessed | tf_op | source)
XLA Modules:
  0.0 45.4 jit_solution(14166002001066044936)
XLA Ops:
  0.0 43.7 %attention_layer.1 = bf16[128,1024]{1,0:T(8,128)(2,1)} custom-call(bf16[128,4096]{1,0:T(8,128)(2,1)} %tokens.1, bf16[4096,1024]{1,0:T(8,128)(2,1)} %w_query.1, bf16[4096,256]{1,0:T(8,128)(2,1)} %w_key.1, bf16[4096,256]{1,0:T(8,128)(2,1)} %w_value.1, bf16[1024,4096]{1,0:T(8,128)(2,1)} %w_out.1, s32[1,128]{1,0:T(1,128)} %bitcast.1, f32[1,128]{1,0:T(1,128)} %constant.2.clone.freqs), custom_call_target="tpu_custom_call" | custom-call | tf_op jit(solution)/shard_map/attention_layer/pallas_call | solution.py:368
  43.7 1.7 %copy.9 = bf16[128,1024]{1,0:T(8,128)(2,1)} copy(bf16[128,1024]{1,0:T(8,128)(2,1)} %attention_layer.1) | data formatting | bytes 524288
